TPU v7x, 32 devices: a whole 2x2x4 slice. The times are simulated.
32 devices in a mesh: attn: 4 (over y, x), expert: 8 (over z, core).
Axes of the slice: x: 2, y: 2, z: 4, core: 2. Of those that a mesh axis runs over, the one named last changes fastest.
Arguments:
- tokens: bfloat16 [1024, 2880], P(('attn', 'expert')), may hold values from -6 to 6
- expert_ids: int32 [1024, 4], P(('attn', 'expert')), may hold values from 0 to 7, all different within a row; in each aligned block of 32 rows (0 to 31, 32 to 63, ...) at most 32 rows name the same one
- gate_probs: float32 [1024, 4], P(('attn', 'expert')), may hold values from 0.05 to 0.6
- shed_blocks: int32 [8], replicated, may hold values from 0 to 4, as said below
- partner: int32 [8], replicated, may hold values from 0 to 7, as said below
- gate_weight: bfloat16 [8, 2880, 2880], P('expert', None, 'attn'), may hold values from -0.109375 to 0.109375
- up_weight: bfloat16 [8, 2880, 2880], P('expert', None, 'attn'), may hold values from -0.109375 to 0.109375
- down_weight: bfloat16 [8, 2880, 2880], P('expert', 'attn'), may hold values from -0.109375 to 0.109375
Outputs:
- moe_out: bfloat16 [1024, 2880], P(('attn', 'expert'))
Inputs may be any that keep to these rules, and one draw needn't show every extreme that they name: `expert_ids`: in the rows of one device, no expert is named by more than 32 rows; the 4 experts of a token differ. `shed_blocks`: some expert has exactly 4. partner pairs the experts: partner[partner[e]] = e and partner[e] != e.
All inputs are finite; a program needn't handle non-finite values.
Results may differ from a plain program's by a relative error of at most 0.0081.
Values may be sent and summed in bfloat16 or wider, within the bound.
A program may use at most 128 MiB of HBM per device.

v0:
```python
import jax
import jax.numpy as jnp
from jax import lax
from jax.sharding import PartitionSpec as P

SHED_MOST = 4


SWISH_SCALE = 1.702


def lookup(table, indices):
    places = jnp.arange(table.shape[0], dtype=jnp.int32)
    return jnp.sum(jnp.where(indices[:, None] == places[None, :], table[None, :], 0), axis=1)


def activate(rows, gate_w, up_w):
    gate_part = jnp.dot(rows, gate_w, preferred_element_type=jnp.float32)
    up_part = jnp.dot(rows, up_w, preferred_element_type=jnp.float32)
    return (gate_part * jax.nn.sigmoid(SWISH_SCALE * gate_part) * (up_part + 1.0)).astype(
        jnp.bfloat16
    )


def on_device(
    tokens, expert_ids, gate_probs, shed_blocks, partner, gate_weight, up_weight, down_weight
):
    tok_rows, model_width = tokens.shape
    top_count = expert_ids.shape[1]
    expert_count = shed_blocks.shape[0]
    group_count = lax.axis_size("attn")
    capacity = tok_rows * top_count * group_count
    block_size = capacity // 8
    most_rows = min(tok_rows, 3 * tok_rows * top_count // expert_count)
    slot_count = 2 * most_rows
    places = jnp.arange(expert_count, dtype=jnp.int32)
    flat_ids = expert_ids.reshape(-1)
    onehot = (flat_ids[:, None] == places[None, :]).astype(jnp.int32)
    counts = jnp.sum(onehot, axis=0)
    local_rank = jnp.sum((jnp.cumsum(onehot, axis=0) - onehot) * onehot, axis=1)
    everyone = lax.all_gather(counts[None, :], ("attn", "expert"), axis=0, tiled=True)
    position_now = lax.axis_index(("attn", "expert"))
    earlier = (jnp.arange(everyone.shape[0], dtype=jnp.int32) < position_now)[:, None]
    offsets = jnp.sum(jnp.where(earlier, everyone, 0), axis=0)
    global_rank = local_rank + jnp.sum(onehot * offsets[None, :], axis=1)
    limit = capacity - block_size * lookup(shed_blocks, partner)
    own_limit = lookup(limit, flat_ids)
    own_shed = lookup(shed_blocks, flat_ids)
    native = global_rank < own_limit
    borrowed = jnp.logical_and(
        jnp.logical_not(native), global_rank < own_limit + block_size * own_shed
    )
    usable = jnp.logical_or(native, borrowed)
    target = jnp.where(usable, flat_ids, -1)
    table_rows = capacity + block_size * SHED_MOST
    target_hot = (target[:, None] == places[None, :]).astype(jnp.int32)
    position = jnp.sum((jnp.cumsum(target_hot, axis=0) - target_hot) * target_hot, axis=1)
    buffer_index = jnp.where(usable, target * slot_count + position, expert_count * slot_count)
    token_rows = jnp.repeat(tokens, top_count, axis=0)
    send_rows = (
        jnp.zeros((expert_count * slot_count, model_width), jnp.bfloat16)
        .at[buffer_index]
        .set(token_rows, mode="drop")
    )
    send_slots = (
        jnp.full((expert_count * slot_count,), table_rows, jnp.int32)
        .at[buffer_index]
        .set(global_rank, mode="drop")
    )
    send_rows = send_rows.reshape(expert_count, slot_count, model_width)
    send_slots = send_slots.reshape(expert_count, slot_count)
    got_rows, got_slots = (
        lax.all_to_all(send_rows, "expert", split_axis=0, concat_axis=0, tiled=True),
        lax.all_to_all(send_slots, "expert", split_axis=0, concat_axis=0, tiled=True),
    )
    local_table = (
        jnp.zeros((table_rows, model_width), jnp.float32)
        .at[got_slots.reshape(-1)]
        .set(got_rows.reshape(-1, model_width).astype(jnp.float32), mode="drop")
    )
    compact = lax.psum(local_table.astype(jnp.bfloat16), "attn")
    gate_own = gate_weight[0]
    up_own = up_weight[0]
    down_own = down_weight[0]
    hidden_own = activate(compact, gate_own, up_own)
    share = lax.psum_scatter(
        jnp.dot(hidden_own, down_own, preferred_element_type=jnp.float32),
        "attn",
        scatter_dimension=0,
        tiled=True,
    )
    results = lax.all_gather(share.astype(jnp.bfloat16), "attn", axis=0, tiled=True)
    answers = results[jnp.minimum(got_slots, table_rows - 1)]
    returned = lax.all_to_all(answers, "expert", split_axis=0, concat_axis=0, tiled=True)
    flat_back = returned.reshape(expert_count * slot_count, model_width)
    picked = flat_back[jnp.minimum(buffer_index, expert_count * slot_count - 1)]
    weights = jnp.where(usable, gate_probs.reshape(-1), 0.0)
    mixed = picked.astype(jnp.float32) * weights[:, None]
    return mixed.reshape(tok_rows, top_count, model_width).sum(axis=1).astype(jnp.bfloat16)


def solution(mesh):
    in_specs = (
        P(("attn", "expert"), None),
        P(("attn", "expert"), None),
        P(("attn", "expert"), None),
        P(),
        P(),
        P("expert", None, "attn"),
        P("expert", None, "attn"),
        P("expert", "attn", None),
    )
    out_specs = P(("attn", "expert"), None)
    return jax.shard_map(
        on_device, mesh=mesh, in_specs=in_specs, out_specs=out_specs, check_vma=False
    )
```

profile of v0, /device:TPU:0, one launch (start us, length us, event | category | flops | bytes accessed | tf_op | source)
XLA Modules:
  0.0 529.1 jit_solution(730793958750302019)
XLA Ops:
  6.5 0.8 copy.15
  7.3 0.1 eq.20
  7.4 0.1 fusion.17
  7.5 0.1 fusion.16
  7.6 0.1 reshape.235
  7.7 0.2 dynamic-update-slice
  8.0 42.0 %all-reduce = s32[256]{0:T(256)S(1)} all-reduce(s32[256]{0:T(256)S(1)} %dynamic-update-slice), channel_id=2, replica_groups=mesh['attn'=4,'expert'=8] {'attn','expert'}, use_global_device_ids=true, to_apply=%add | all-reduce | flops 256 | bytes 2048
  49.9 0.1 reshape.282
  50.0 0.2 reduce_window_sum.17
  50.2 0.9 select_reduce_fusion.6
  51.1 0.1 select_reduce_fusion.5
  51.1 0.9 select_reduce_fusion.1
  52.0 0.1 fusion.15
  52.1 0.2 reduce_window_sum.18
  52.3 0.2 select_reduce_fusion
  52.5 1.0 scatter_custom_fusion
  53.5 0.7 all_to_all.12
  54.2 3.6 all-to-all-start
  57.8 1.1 broadcast_in_dim.95
  58.9 0.4 reshape.270
  59.3 3.8 scatter_custom_fusion.1
  63.0 0.2 all-to-all-done
  63.3 4.9 all-to-all-start.1
  68.2 0.5 broadcast.220
  68.7 0.7 broadcast_minimum_fusion
  69.4 0.1 reshape.236
  69.5 67.4 %all-to-all-done.1 = bf16[8,64,2880]{2,1,0:T(8,128)(2,1)S(1)} async-done(((bf16[8,64,2880]{2,1,0:T(8,128)(2,1)}), bf16[8,64,2880]{2,1,0:T(8,128)(2,1)S(1)}, u32[]{:S(2)}, u32[]{:S(2)}) %all-to-all-start.1) | async-done | bytes 2949152 | tf_op jit(solution)/shard_map/all_to_all | solution.py:73
  136.8 8.4 %scatter_custom_fusion.2 = f32[768,2880]{1,0:T(8,128)} fusion(s32[512]{0:T(512)S(1)} %bitcast.54, bf16[512,2880]{1,0:T(8,128)(2,1)S(1)} %bitcast.51, f32[]{:T(128)} %constant.14.clone.1), kind=kCustom, calls=%fused_computation.5 | custom fusion | flops 1474560 | bytes 11862020 | tf_op jit(solution)/shard_map/scatter | solution.py:79
  145.3 6.1 %convert_element_type.35 = bf16[768,2880]{1,0:T(8,128)(2,1)} convert(f32[768,2880]{1,0:T(8,128)} %scatter_custom_fusion.2) | non-fusion elementwise | flops 2211840 | bytes 13271040 | tf_op jit(solution)/shard_map/convert_element_type | solution.py:81
  151.4 0.2 reduce-scatter.2.cloned.1.call-start
  151.6 107.7 %all-reduce.3.cloned.1.call-done = bf16[768,2880]{1,0:T(8,128)(2,1)} async-done(((bf16[768,2880]{1,0:T(8,128)(2,1)}), bf16[768,2880]{1,0:T(8,128)(2,1)}) %all-reduce.3.cloned.1.call-update) | async-done | bytes 4423696 | tf_op jit(solution)/shard_map/psum | solution.py:81
  259.3 6.8 %fusion.5 = f32[768,720]{0,1:T(8,128)S(1)} fusion(bf16[768,2880]{1,0:T(8,128)(2,1)} %all-reduce.3.cloned.1.call-done, bf16[1,2880,720]{1,2,0:T(8,128)(2,1)} %param.14), kind=kOutput, calls=%fused_computation.10 | convolution fusion | flops 3185049600 | bytes 10782720 | tf_op jit(solution)/shard_map/dot_general | solution.py:19
  266.1 18.0 %fusion.3 = f32[768,2880]{1,0:T(8,128)} fusion(bf16[1,720,2880]{2,1,0:T(8,128)(2,1)} %param.15, f32[768,720]{0,1:T(8,128)S(1)} %fusion.5, bf16[768,2880]{1,0:T(8,128)(2,1)} %all-reduce.3.cloned.1.call-done, bf16[1,2880,720]{1,2,0:T(8,128)(2,1)} %param.13), kind=kOutput, calls=%fused_computation.8 | convolution fusion | flops 6374522880 | bytes 23777280 | tf_op jit(solution)/shard_map/dot_general | solution.py:87
  284.1 0.3 all-gather.3.cloned.1.call-start
  284.4 91.6 %reduce-scatter.2.cloned.1.call-done = f32[192,2880]{1,0:T(8,128)} async-done(((f32[768,2880]{1,0:T(8,128)}), f32[192,2880]{1,0:T(8,128)}) %reduce-scatter.2.cloned.1.call-update) | async-done | bytes 2211856 | tf_op jit(solution)/shard_map/reduce_scatter | solution.py:86
  376.0 2.8 convert_element_type.37
  378.8 0.1 reshape.244
  378.9 55.4 %all-gather.3.cloned.1.call-done = bf16[768,2880]{1,0:T(8,128)(2,1)} async-done(((bf16[192,2880]{1,0:T(8,128)(2,1)}), bf16[768,2880]{1,0:T(8,128)(2,1)}) %all-gather.3.cloned.1.call-update) | async-done | bytes 4423696 | tf_op jit(solution)/shard_map/all_gather | solution.py:92
  434.2 9.6 %gather_fusion = bf16[512,2880]{1,0:T(8,128)(2,1)} fusion(bf16[768,2880]{1,0:T(8,128)(2,1)} %all-gather.3.cloned.1.call-done, s32[1024]{0:T(1024)S(1)} %pad_clamp_fusion.1), kind=kCustom, calls=%fused_computation | custom fusion | bytes 5900288 | tf_op jit(solution)/shard_map/gather | solution.py:93
  443.8 4.7 all-to-all-start.2
  448.6 0.1 add.134
  448.7 0.1 reduce_sum.97
  448.8 0.1 mul.98
  448.9 0.1 copy.17
  449.0 68.3 %all-to-all-done.2 = bf16[8,64,2880]{2,1,0:T(8,128)(2,1)S(1)} async-done(((bf16[8,64,2880]{2,1,0:T(8,128)(2,1)}), bf16[8,64,2880]{2,1,0:T(8,128)(2,1)S(1)}, u32[]{:S(2)}, u32[]{:S(2)}) %all-to-all-start.2) | async-done | bytes 2949152 | tf_op jit(solution)/shard_map/all_to_all | solution.py:94
  517.3 1.9 gather_fusion.1
  519.2 1.7 reshape.241
  520.8 1.7 multiply_reduce_fusion
  (17 shorter events, 0.2 us)
Async XLA Ops:
  54.2 9.1 %all-to-all-start = ((s32[8,1,64]{2,1,0:T(1,128)}), s32[8,1,64]{2,1,0:T(1,128)S(1)}, u32[]{:S(2)}, u32[]{:S(2)}) async-start(s32[8,1,64]{2,1,0:T(1,128)} %all_to_all.12), calls=%async_computation | async-start | bytes 8192 | tf_op jit(solution)/shard_map/all_to_all | solution.py:74
  63.3 73.6 %all-to-all-start.1 = ((bf16[8,64,2880]{2,1,0:T(8,128)(2,1)}), bf16[8,64,2880]{2,1,0:T(8,128)(2,1)S(1)}, u32[]{:S(2)}, u32[]{:S(2)}) async-start(bf16[8,64,2880]{2,1,0:T(8,128)(2,1)} %bitcast.6), calls=%async_computation.1 | async-start | bytes 6029312 | tf_op jit(solution)/shard_map/all_to_all | solution.py:73
  68.2 191.2 %all-reduce.3.cloned.1.call-start = ((), (), s32[]{:S(2)}) async-start(), calls=%async_computation.4 | async-start | bytes 9043968 | tf_op jit(solution)/shard_map/psum | solution.py:81
  151.4 224.6 %reduce-scatter.2.cloned.1.call-start = ((), (), s32[]{:S(2)}) async-start(), calls=%async_computation.5 | async-start | bytes 11304960 | tf_op jit(solution)/shard_map/reduce_scatter | solution.py:86
  284.1 150.1 %all-gather.3.cloned.1.call-start = ((), (), s32[]{:S(2)}) async-start(), calls=%async_computation.6 | async-start | bytes 5652480 | tf_op jit(solution)/shard_map/all_gather | solution.py:92
  443.8 5.1 copy-start
  443.8 73.4 %all-to-all-start.2 = ((bf16[8,64,2880]{2,1,0:T(8,128)(2,1)}), bf16[8,64,2880]{2,1,0:T(8,128)(2,1)S(1)}, u32[]{:S(2)}, u32[]{:S(2)}) async-start(bf16[8,64,2880]{2,1,0:T(8,128)(2,1)} %bitcast.52), calls=%async_computation.3 | async-start | bytes 6029312 | tf_op jit(solution)/shard_map/all_to_all | solution.py:94
Sparse Core Ops, SparseCore 0:
  151.5 107.7 all-reduce.2
  284.3 91.6 reduce-scatter.1
  378.9 55.2 all-gather.2
where the time goes:
time: 530 us; the launch traced here: 529 us
  waiting for transfers between devices  391 us (74%)
  blocking collectives  42 us (8%)
  matrix products  24.8 us (5%)
  local copies, waits for them, and re-layouts  22.4 us (4%)
  other arithmetic  22.3 us (4%)
  starting transfers between devices  13.7 us (3%)
  between operations  13.3 us (3%)
    psum x1, waiting for transfers between devices, on_device(): compact = lax.psum(local_table.astype(jnp.bfloat16), 'attn')  108 us
    reduce_scatter x1, waiting for transfers between devices, on_device(): lax.psum_scatter(jnp.dot(hidden_own, down_own, preferred_element_type=jnp...  91.6 us
    all_to_all x1, waiting for transfers between devices, on_device(): lax.all_to_all(answers, 'expert', split_axis=0, concat_axis=0, tiled=True)  68.3 us
    all_to_all x1, waiting for transfers between devices, on_device(): lax.all_to_all(send_rows, 'expert', split_axis=0, concat_axis=0, tiled=True)  67.4 us
    all_gather x1, waiting for transfers between devices, on_device(): lax.all_gather(share.astype(jnp.bfloat16), 'attn', axis=0, tiled=True)  55.4 us
    unnamed x1, blocking collectives  42 us
    dot_general x1, matrix products, on_device(): jnp.dot(hidden_own, down_own, preferred_element_type=jnp.float32)  18 us
  transfers between devices with their start and end apart: 6, of which 6 were waited for; matrix products, arithmetic and copies ran while one was open for 1% of the time, Pallas kernels for 0%

commit v1 on v0

v1 whole, which is shorter than its diff:
```python
import jax
import jax.numpy as jnp
from jax import lax
from jax.sharding import PartitionSpec as P

SHED_MOST = 4


SWISH_SCALE = 1.702


def lookup(table, indices):
    places = jnp.arange(table.shape[0], dtype=jnp.int32)
    return jnp.sum(jnp.where(indices[:, None] == places[None, :], table[None, :], 0), axis=1)


def row_weights(all_ids, all_probs, shed_blocks, partner, capacity, block_size):
    me = lax.axis_index("expert").astype(jnp.int32)
    named = all_ids == me
    mask = jnp.any(named, axis=1).astype(jnp.int32)
    rank = jnp.cumsum(mask) - mask
    other = lookup(partner, me[None])
    bound = (
        capacity - block_size * lookup(shed_blocks, other) + block_size * lookup(shed_blocks, me[None])
    )
    weight = jnp.sum(jnp.where(named, all_probs, 0.0), axis=1)
    return jnp.where(rank < bound, weight, 0.0)


def on_device(
    tokens, expert_ids, gate_probs, shed_blocks, partner, gate_weight, up_weight, down_weight
):
    tok_rows, model_width = tokens.shape
    top_count = expert_ids.shape[1]
    capacity = tok_rows * top_count * lax.axis_size("attn")
    block_size = capacity // 8
    both = ("attn", "expert")
    all_ids = lax.all_gather(expert_ids, both, axis=0, tiled=True)
    all_probs = lax.all_gather(gate_probs, both, axis=0, tiled=True)
    rows = lax.all_gather(tokens, both, axis=0, tiled=True)
    weight = row_weights(all_ids, all_probs, shed_blocks, partner, capacity, block_size)
    gate_part = jnp.dot(rows, gate_weight[0], preferred_element_type=jnp.float32)
    up_part = jnp.dot(rows, up_weight[0], preferred_element_type=jnp.float32)
    hidden = gate_part * jax.nn.sigmoid(SWISH_SCALE * gate_part) * (up_part + 1.0)
    hidden = (hidden * weight[:, None]).astype(jnp.bfloat16)
    share = jnp.dot(hidden, down_weight[0], preferred_element_type=jnp.float32).astype(jnp.bfloat16)
    share = lax.psum_scatter(share, "attn", scatter_dimension=0, tiled=True)
    return lax.psum_scatter(share, "expert", scatter_dimension=0, tiled=True)


def solution(mesh):
    in_specs = (
        P(("attn", "expert"), None),
        P(("attn", "expert"), None),
        P(("attn", "expert"), None),
        P(),
        P(),
        P("expert", None, "attn"),
        P("expert", None, "attn"),
        P("expert", "attn", None),
    )
    out_specs = P(("attn", "expert"), None)
    return jax.shard_map(
        on_device, mesh=mesh, in_specs=in_specs, out_specs=out_specs, check_vma=False
    )
```

time: 530 us -> 227 us (0.43)
  waiting for transfers between devices: 391 us -> 99.1 us
  blocking collectives: 42 us -> 82 us
  local copies, waits for them, and re-layouts: 22.4 us -> 2.97 us
  other arithmetic: 22.3 us -> 3.78 us
  starting transfers between devices: 13.7 us -> 0.08 us
    all_to_all x3 -> x0, waiting for transfers between devices: 136 us -> none  [the longest x1 68.3 us: on_device(): lax.all_to_all(answers, 'expert', split_axis=0, concat_axis=0, tiled=True)]
    psum x1 -> x0, waiting for transfers between devices: 108 us -> none  [on_device(): compact = lax.psum(local_table.astype(jnp.bfloat16), 'attn')]
    all_gather x0 -> x2, blocking collectives: none -> 82 us  [the longest x1 44.1 us: on_device(): all_ids = lax.all_gather(expert_ids, both, axis=0, tiled=True)]
    all_gather x1, waiting for transfers between devices: 55.4 us -> 0.01 us  [on_device(): rows = lax.all_gather(tokens, both, axis=0, tiled=True)]
    unnamed x1 -> x0, blocking collectives: 42 us -> none
    all_to_all x3 -> x0, starting transfers between devices: 13.2 us -> none  [the longest x1 4.86 us: on_device(): lax.all_to_all(send_rows, 'expert', split_axis=0, concat_axis=0, tiled=True)]
    gather x2 -> x0, local copies, waits for them, and re-layouts: 11.5 us -> none  [the longest x1 9.62 us: on_device(): answers = results[jnp.minimum(got_slots, table_rows - 1)]]
    convert_element_type x4 -> x1, other arithmetic: 9.03 us -> 0.01 us  [row_weights(): mask = jnp.any(named, axis=1).astype(jnp.int32)]
  transfers between devices with their start and end apart: 6 -> 3, of which waited for: 6 -> 2; matrix products, arithmetic and copies ran while one was open for 1% -> 2% of each run, Pallas kernels for 0% -> 0%
where the time goes in v1:
time: 227 us
  waiting for transfers between devices  99.1 us (44%)
  blocking collectives  82 us (36%)
  matrix products  24.4 us (11%)
  between operations  14.4 us (6%)
  other arithmetic  3.78 us (2%)
  local copies, waits for them, and re-layouts  2.97 us (1%)
    reduce_scatter x1, waiting for transfers between devices, on_device(): share = lax.psum_scatter(share, 'attn', scatter_dimension=0, tiled=True)  64.1 us
    all_gather x1, blocking collectives, on_device(): all_ids = lax.all_gather(expert_ids, both, axis=0, tiled=True)  44.1 us
    all_gather x1, blocking collectives, on_device(): all_probs = lax.all_gather(gate_probs, both, axis=0, tiled=True)  37.9 us
    reduce_scatter x1, waiting for transfers between devices, on_device(): return lax.psum_scatter(share, 'expert', scatter_dimension=0, tiled=True)  34.3 us
    dot_general x1, matrix products, on_device(): jnp.dot(hidden, down_weight[0], preferred_element_type=jnp.float32)  16.3 us
    dot_general x1, matrix products, on_device(): up_part = jnp.dot(rows, up_weight[0], preferred_element_type=jnp.float32)  8.09 us
  transfers between devices with their start and end apart: 3, of which 2 were waited for; matrix products, arithmetic and copies ran while one was open for 2% of the time, Pallas kernels for 0%

profile of v1, /device:TPU:0, one launch (start us, length us, event | category | flops | bytes accessed | tf_op | source)
XLA Modules:
  0.0 226.7 jit_solution(15309892988968563415)
XLA Ops:
  6.5 0.0 all-gather.4.cloned.1.call-start
  6.5 0.7 all-gather.4.cloned.1.call-update
  7.3 0.0 reduce-scatter.5.cloned.1.call-start
  7.3 44.1 %all-gather = s32[32,32,4]{1,2,0:T(4,128)S(1)} all-gather(s32[1,32,4]{1,2,0:T(4,128)} %bitcast.24), channel_id=1, replica_groups=mesh['attn'=4,'expert'=8] {'attn','expert'}, dimensions={0}, use_global_device_ids=true | all-gather | bytes 16896 | tf_op jit(solution)/shard_map/all_gather | solution.py:38
  51.4 0.1 fusion.19
  51.4 0.1 reshape.58
  51.5 0.1 reshape.68
  51.6 1.3 fusion.14
  52.9 2.0 fusion.15
  56.1 0.3 reduce-window.9
  56.4 0.1 slice.7
  56.5 37.9 %all-gather.1 = f32[32,32,4]{1,2,0:T(4,128)S(1)} all-gather(f32[1,32,4]{1,2,0:T(4,128)} %bitcast.25), channel_id=1, replica_groups=mesh['attn'=4,'expert'=8] {'attn','expert'}, dimensions={0}, use_global_device_ids=true | all-gather | bytes 16896 | tf_op jit(solution)/shard_map/all_gather | solution.py:39
  94.4 0.1 select_reduce_fusion
  94.5 0.1 reshape.70
  94.6 0.1 slice_reduce_fusion
  94.7 0.1 fusion.13
  94.8 0.0 all-gather.4.cloned.1.call-done
  94.8 8.1 %fusion.1 = f32[1024,720]{0,1:T(8,128)S(1)} fusion(bf16[1024,2880]{1,0:T(8,128)(2,1)} %all-gather.4.cloned.1.call-done, bf16[1,2880,720]{1,2,0:T(8,128)(2,1)} %param.14), kind=kOutput, calls=%fused_computation.2 | convolution fusion | flops 4246732800 | bytes 12994560 | tf_op jit(solution)/shard_map/dot_general | solution.py:43
  102.9 16.3 %convolution_convert_fusion = bf16[1024,2880]{0,1:T(8,128)(2,1)} fusion(bf16[1,720,2880]{2,1,0:T(8,128)(2,1)} %param.15, f32[1024,720]{0,1:T(8,128)S(1)} %fusion.1, bf16[1024,2880]{1,0:T(8,128)(2,1)} %all-gather.4.cloned.1.call-done, bf16[1,2880,720]{1,2,0:T(8,128)(2,1)} %param.13, f32[1024]{0:T(1024)S(1)} %fusion.13), kind=kOutput, calls=%fused_computation | convolution fusion | flops 8503050240 | bytes 23044096 | tf_op jit(solution)/shard_map/dot_general | solution.py:46
  119.1 0.0 reduce-scatter.5.cloned.1.call-update
  119.2 0.0 reduce-scatter.7.cloned.1.call-start
  119.2 64.1 %reduce-scatter.5.cloned.1.call-done = bf16[256,2880]{0,1:T(8,128)(2,1)} async-done(((bf16[1024,2880]{0,1:T(8,128)(2,1)}), bf16[256,2880]{0,1:T(8,128)(2,1)}) %reduce-scatter.5.cloned.1.call-update) | async-done | bytes 1474576 | tf_op jit(solution)/shard_map/reduce_scatter | solution.py:47
  183.3 2.6 %copy.12 = bf16[256,2880]{1,0:T(8,128)(2,1)} copy(bf16[256,2880]{0,1:T(8,128)(2,1)} %reduce-scatter.5.cloned.1.call-done) | data formatting | bytes 2949120
  185.9 0.0 reduce-scatter.7.cloned.1.call-update
  185.9 34.3 %reduce-scatter.7.cloned.1.call-done = bf16[32,2880]{1,0:T(8,128)(2,1)} async-done(((bf16[256,2880]{1,0:T(8,128)(2,1)}), bf16[32,2880]{1,0:T(8,128)(2,1)}) %reduce-scatter.7.cloned.1.call-update) | async-done | bytes 184336 | tf_op jit(solution)/shard_map/reduce_scatter | solution.py:48
  (2 shorter events, 0.0 us)
Async XLA Ops:
  6.5 88.2 %all-gather.4.cloned.1.call-start = ((), (), s32[]{:S(2)}) async-start(), calls=%async_computation.2 | async-start | bytes 6217728 | tf_op jit(solution)/shard_map/all_gather | solution.py:40
  7.3 176.0 %reduce-scatter.5.cloned.1.call-start = ((), (), s32[]{:S(2)}) async-start(), calls=%async_computation.3 | async-start | bytes 7372800 | tf_op jit(solution)/shard_map/reduce_scatter | solution.py:47
  119.2 101.0 %reduce-scatter.7.cloned.1.call-start = ((), (), s32[]{:S(2)}) async-start(), calls=%async_computation.4 | async-start | bytes 1695744 | tf_op jit(solution)/shard_map/reduce_scatter | solution.py:48
Sparse Core Ops, SparseCore 0:
  10.2 70.8 all-gather.3
  119.3 63.9 reduce-scatter.4
  186.0 34.1 reduce-scatter.6

commit v2 on v1

v2 whole, which is shorter than its diff:
```python
import functools

import jax
import jax.numpy as jnp
from jax import lax
from jax.experimental import pallas as pl
from jax.experimental.pallas import tpu as pltpu
from jax.sharding import PartitionSpec as P

SHED_MOST = 4


SWISH_SCALE = 1.702
LANES = 128
VMEM_BYTES = 60 * 2**20
MESH = pl.DeviceIdType.MESH

OWN_X, OWN_Y, OWN_C, FWD_Y, FWD_X, PASS_X, PASS_Y, PASS_D = range(8)
SUM_C, HALF_X, HALF_Y, FULL_X, FULL_Y, BACK_Z, OUT_Z = range(8, 15)
META_Z, META_A, META_C = range(15, 18)
KINDS = 18


def lookup(table, indices):
    places = jnp.arange(table.shape[0], dtype=jnp.int32)
    return jnp.sum(jnp.where(indices[:, None] == places[None, :], table[None, :], 0), axis=1)


def served_rows(shed_blocks, partner, capacity):
    me = lax.axis_index("expert").astype(jnp.int32)[None]
    other = lookup(partner, me)
    block_size = capacity // 8
    return capacity + block_size * (lookup(shed_blocks, me) - lookup(shed_blocks, other))


def activate(gate_part, up_part, weight):
    return (gate_part * jax.nn.sigmoid(SWISH_SCALE * gate_part) * (up_part + 1.0) * weight).astype(
        jnp.bfloat16
    )


def kernel(
    tokens,
    meta,
    bound,
    gate_hbm,
    up_hbm,
    down_hbm,
    out,
    x,
    m,
    wcol,
    part,
    core_in,
    total,
    half_in,
    full_in,
    z_out,
    z_in,
    kept,
    gate,
    up,
    down,
    send_sem,
    recv_sem,
    load_sem,
):
    planes = x.shape[0]
    rows, width = tokens.shape
    half = rows // 2
    top = meta.shape[0] // 2
    a = lax.axis_index("attn")
    e = lax.axis_index("expert")
    z, c = e // 2, e % 2

    def xor(value, bits):
        result = value
        for bit in (1, 2, 4, 8):
            if bits & bit:
                result = result + bit - 2 * bit * ((value // bit) % 2)
        return result

    xn, yn, dn = xor(a, 1), xor(a, 2), xor(a, 3)
    oc = 1 - c
    to_x, to_y, to_d, to_c = (xn, e), (yn, e), (dn, e), (a, z * 2 + oc)

    def plane(s):
        low = (z % 2 + s % 2) % 2
        high = (z // 2 + s // 2) % 2
        return high * 2 + low

    def copy(kind, s, src, dst, to):
        return pltpu.make_async_remote_copy(
            src_ref=src,
            dst_ref=dst,
            send_sem=send_sem.at[kind, s],
            recv_sem=recv_sem.at[kind, s],
            device_id=to,
            device_id_type=MESH,
        )

    def same(kind, s, ref, to):
        return copy(kind, s, ref, ref, to)

    lo, hi = pl.ds(0, half), pl.ds(half, half)

    def make(kind, s):
        p = plane(s)
        if kind == OUT_Z:
            return copy(kind, s, tokens, x.at[z, c, a], (a, p * 2 + c))
        if kind == OWN_X:
            return same(kind, s, x.at[p, c, a], to_x)
        if kind == OWN_Y:
            return same(kind, s, x.at[p, c, a], to_y)
        if kind == OWN_C:
            return same(kind, s, x.at[p, c, a], to_c)
        if kind == FWD_Y:
            return same(kind, s, x.at[p, c, xn, lo], to_y)
        if kind == FWD_X:
            return same(kind, s, x.at[p, c, yn, hi], to_x)
        if kind == PASS_X:
            return same(kind, s, x.at[p, c, xn], to_c)
        if kind == PASS_Y:
            return same(kind, s, x.at[p, c, yn], to_c)
        if kind == PASS_D:
            return same(kind, s, x.at[p, c, dn], to_c)
        if kind == SUM_C:
            return copy(kind, s, part.at[s, oc], core_in.at[s], to_c)
        if kind == HALF_X:
            return copy(kind, s, total.at[s, dn, lo], half_in.at[s, 0], to_x)
        if kind == HALF_Y:
            return copy(kind, s, total.at[s, dn, hi], half_in.at[s, 1], to_y)
        if kind == FULL_X:
            return copy(kind, s, total.at[s, xn], full_in.at[s, 0], to_x)
        if kind == FULL_Y:
            return copy(kind, s, total.at[s, yn], full_in.at[s, 1], to_y)
        if kind == BACK_Z:
            return copy(kind, s, z_out.at[s], z_in.at[s], (a, p * 2 + c))
        if kind == META_Z:
            return copy(kind, s, meta, m.at[a, z, c], (a, p * 2 + c))
        if kind == META_A:
            to = (to_x, to_x, to_y, to_d)[s]
            return same(kind, s, m.at[a, :, c], to)
        if kind == META_C:
            return same(kind, s, m.at[:, :, c], to_c)

    def start(s, *kinds):
        for kind in kinds:
            make(kind, s).start()

    def arrived(s, *kinds):
        for kind in kinds:
            make(kind, s).wait_recv()

    def sent(s, *kinds):
        for kind in kinds:
            make(kind, s).wait_send()

    def widen(ref):
        return ref[...].astype(jnp.float32)

    barrier = pltpu.get_barrier_semaphore()
    peers = [to_x, to_y, to_d, to_c] + [(a, plane(s) * 2 + c) for s in range(1, planes)]
    for peer in peers:
        pl.semaphore_signal(barrier, inc=1, device_id=peer, device_id_type=MESH)

    own = pltpu.make_async_copy(tokens, x.at[z, c, a], load_sem.at[3])
    own_meta = pltpu.make_async_copy(meta, m.at[a, z, c], load_sem.at[4])
    loads = [
        pltpu.make_async_copy(gate_hbm.at[0], gate, load_sem.at[0]),
        pltpu.make_async_copy(up_hbm.at[0], up, load_sem.at[1]),
        pltpu.make_async_copy(down_hbm.at[0], down, load_sem.at[2]),
    ]
    own.start()
    own_meta.start()
    for load in loads:
        load.start()
    pl.semaphore_wait(barrier, len(peers))

    for s in range(1, planes):
        start(s, META_Z)
    own.wait()
    own_meta.wait()
    start(0, OWN_X, OWN_Y, OWN_C)
    for s in range(1, planes):
        start(s, OUT_Z)

    def stage_own(s):
        arrived(s, OUT_Z)
        start(s, OWN_X, OWN_Y, OWN_C)

    def stage_forward(s):
        arrived(s, OWN_X)
        start(s, FWD_Y, PASS_X)
        arrived(s, OWN_Y)
        start(s, FWD_X, PASS_Y)

    for s in range(1, planes):
        arrived(s, META_Z)
    for s in range(1, 4):
        start(s, META_A)
    stage_forward(0)
    for s in range(1, 4):
        arrived(s, META_A)
    start(0, META_C)
    stage_own(1)
    arrived(0, META_C)

    def row_weights():
        table = m[...].reshape(m.shape[0] * m.shape[1] * m.shape[2], 2 * top, LANES)
        blocks = table.shape[0]
        named = table[:, :top, :] == e.astype(jnp.float32)
        mask = jnp.sum(jnp.where(named, 1.0, 0.0), axis=1)
        prob = jnp.sum(jnp.where(named, table[:, top:, :], 0.0), axis=1)
        mask16 = mask.astype(jnp.bfloat16)
        i = lax.broadcasted_iota(jnp.int32, (LANES, LANES), 0)
        j = lax.broadcasted_iota(jnp.int32, (LANES, LANES), 1)
        before = jnp.where(i < j, 1.0, 0.0).astype(jnp.bfloat16)
        inside = jnp.dot(mask16, before, preferred_element_type=jnp.float32)
        i = lax.broadcasted_iota(jnp.int32, (blocks, blocks), 0)
        j = lax.broadcasted_iota(jnp.int32, (blocks, blocks), 1)
        earlier = jnp.where(j < i, 1.0, 0.0).astype(jnp.bfloat16)
        ahead = jnp.dot(earlier, mask16, preferred_element_type=jnp.float32)
        rank = inside + jnp.sum(ahead, axis=1, keepdims=True)
        weight = jnp.where(rank < bound[...], prob, 0.0)
        i = lax.broadcasted_iota(jnp.int32, (rows, LANES), 0)
        j = lax.broadcasted_iota(jnp.int32, (rows, LANES), 1)
        for aa in range(m.shape[0]):
            for zz in range(m.shape[1]):
                for cc in range(2):
                    block = (aa * m.shape[1] + zz) * 2 + cc
                    spread = jnp.where(i == j, weight[block : block + 1, :], 0.0)
                    wcol[zz, cc, aa] = jnp.sum(spread, axis=1, keepdims=True)

    row_weights()
    for load in loads:
        load.wait()

    def compute(s):
        p = plane(s)
        count = 2 * m.shape[0] * rows
        xs = x[p].reshape(count, width)
        gate_part = jnp.dot(xs, gate[...], preferred_element_type=jnp.float32)
        up_part = jnp.dot(xs, up[...], preferred_element_type=jnp.float32)
        hidden = activate(gate_part, up_part, wcol[p].reshape(count, 1))
        step = 8 * LANES
        for first in range(0, width, step):
            cols = slice(first, min(first + step, width))
            share = jnp.dot(hidden, down[:, cols], preferred_element_type=jnp.float32)
            part[s, :, :, :, cols] = share.astype(jnp.bfloat16).reshape(
                2, m.shape[0], rows, cols.stop - cols.start
            )

    def body(t, carry):
        @pl.when(t < planes)
        def _():
            arrived(t, FWD_Y, FWD_X)
            start(t, PASS_D)
            arrived(t, OWN_C, PASS_X, PASS_Y, PASS_D)

        @pl.when(t + 2 < planes)
        def _():
            stage_own(t + 2)

        @pl.when(t < planes)
        def _():
            compute(t)
            start(t, SUM_C)

        @pl.when(t + 1 < planes)
        def _():
            stage_forward(t + 1)

        @pl.when(t < planes)
        def _():
            arrived(t, SUM_C)
            total[t] = (widen(part.at[t, c]) + widen(core_in.at[t])).astype(jnp.bfloat16)
            start(t, HALF_X, HALF_Y)

        @pl.when(jnp.logical_and(t >= 1, t < planes + 1))
        def _():
            s = t - 1
            arrived(s, HALF_X, HALF_Y)
            low = widen(total.at[s, yn, lo]) + widen(half_in.at[s, 0])
            total[s, yn, lo] = low.astype(jnp.bfloat16)
            start(s, FULL_Y)
            high = widen(total.at[s, xn, hi]) + widen(half_in.at[s, 1])
            total[s, xn, hi] = high.astype(jnp.bfloat16)
            start(s, FULL_X)

        @pl.when(t >= 2)
        def _():
            s = t - 2
            arrived(s, FULL_X, FULL_Y)
            value = widen(total.at[s, a]) + widen(full_in.at[s, 0]) + widen(full_in.at[s, 1])

            @pl.when(s == 0)
            def _():
                kept[...] = value

            @pl.when(s > 0)
            def _():
                z_out[s] = value.astype(jnp.bfloat16)
                start(s, BACK_Z)

        return carry

    lax.fori_loop(0, planes + 2, body, 0)

    value = kept[...]
    for s in range(1, planes):
        arrived(s, BACK_Z)
        value = value + widen(z_in.at[s])
    out[...] = value.astype(out.dtype)

    def drain(s, carry):
        sent(s, *range(OWN_X, BACK_Z))

        @pl.when(s > 0)
        def _():
            sent(s, BACK_Z, OUT_Z, META_Z)

        return carry

    lax.fori_loop(0, planes, drain, 0)
    for s in range(1, 4):
        sent(s, META_A)
    sent(0, META_C)


def fused_bytes(group_count, planes, rows, width, hidden):
    wide = -(-width // LANES) * LANES
    block = rows * wide * 2
    weights = 2 * width * (-(-hidden // LANES) * LANES) * 2 + hidden * wide * 2
    return weights + planes * group_count * block * (2 + 2 + 1 + 1 + 2) + 12 * 2**20


def fused(tokens, meta, bound, gate_weight, up_weight, down_weight, group_count, planes):
    rows, width = tokens.shape
    hidden = gate_weight.shape[2]
    bf16, f32 = jnp.bfloat16, jnp.float32
    vmem = pl.BlockSpec(memory_space=pltpu.VMEM)
    hbm = pl.BlockSpec(memory_space=pl.ANY)
    return pl.pallas_call(
        kernel,
        out_shape=jax.ShapeDtypeStruct((rows, width), bf16),
        in_specs=[vmem, vmem, vmem, hbm, hbm, hbm],
        out_specs=vmem,
        scratch_shapes=[
            pltpu.VMEM((planes, 2, group_count, rows, width), bf16),
            pltpu.VMEM((group_count, planes, 2) + meta.shape, f32),
            pltpu.VMEM((planes, 2, group_count, rows, 1), f32),
            pltpu.VMEM((planes, 2, group_count, rows, width), bf16),
            pltpu.VMEM((planes, group_count, rows, width), bf16),
            pltpu.VMEM((planes, group_count, rows, width), bf16),
            pltpu.VMEM((planes, 2, rows // 2, width), bf16),
            pltpu.VMEM((planes, 2, rows, width), bf16),
            pltpu.VMEM((planes, rows, width), bf16),
            pltpu.VMEM((planes, rows, width), bf16),
            pltpu.VMEM((rows, width), f32),
            pltpu.VMEM((width, hidden), bf16),
            pltpu.VMEM((width, hidden), bf16),
            pltpu.VMEM((hidden, width), bf16),
            pltpu.SemaphoreType.DMA((KINDS, planes)),
            pltpu.SemaphoreType.DMA((KINDS, planes)),
            pltpu.SemaphoreType.DMA((5,)),
        ],
        compiler_params=pltpu.CompilerParams(
            collective_id=0, has_side_effects=True, vmem_limit_bytes=VMEM_BYTES
        ),
    )(tokens, meta, bound, gate_weight, up_weight, down_weight)


def gathered(tokens, expert_ids, gate_probs, bound, gate_weight, up_weight, down_weight):
    both = ("attn", "expert")
    all_ids = lax.all_gather(expert_ids, both, axis=0, tiled=True)
    all_probs = lax.all_gather(gate_probs, both, axis=0, tiled=True)
    rows = lax.all_gather(tokens, both, axis=0, tiled=True)
    named = all_ids == lax.axis_index("expert").astype(jnp.int32)
    mask = jnp.any(named, axis=1).astype(jnp.int32)
    rank = jnp.cumsum(mask) - mask
    weight = jnp.sum(jnp.where(named, all_probs, 0.0), axis=1)
    weight = jnp.where(rank < bound, weight, 0.0)
    gate_part = jnp.dot(rows, gate_weight[0], preferred_element_type=jnp.float32)
    up_part = jnp.dot(rows, up_weight[0], preferred_element_type=jnp.float32)
    hidden = activate(gate_part, up_part, weight[:, None])
    share = jnp.dot(hidden, down_weight[0], preferred_element_type=jnp.float32).astype(jnp.bfloat16)
    share = lax.psum_scatter(share, "attn", scatter_dimension=0, tiled=True)
    return lax.psum_scatter(share, "expert", scatter_dimension=0, tiled=True)


def on_device(
    tokens, expert_ids, gate_probs, shed_blocks, partner, gate_weight, up_weight, down_weight
):
    rows, width = tokens.shape
    group_count, expert_count = lax.axis_size("attn"), lax.axis_size("expert")
    top_count = expert_ids.shape[1]
    planes = expert_count // 2
    bound = served_rows(shed_blocks, partner, rows * top_count * group_count)
    fits = fused_bytes(group_count, planes, rows, width, gate_weight.shape[2]) <= VMEM_BYTES
    if group_count != 4 or planes != 4 or rows % 32 or rows > LANES or not fits:
        return gathered(
            tokens, expert_ids, gate_probs, bound, gate_weight, up_weight, down_weight
        )
    ids = jnp.pad(
        expert_ids.T.astype(jnp.float32), ((0, 0), (0, LANES - rows)), constant_values=-1.0
    )
    probs = jnp.pad(gate_probs.T, ((0, 0), (0, LANES - rows)))
    meta = jnp.concatenate([ids, probs], axis=0)
    bound = jnp.broadcast_to(bound.astype(jnp.float32)[:, None], (1, LANES))
    return fused(
        tokens, meta, bound, gate_weight, up_weight, down_weight, group_count, planes
    )


def solution(mesh):
    in_specs = (
        P(("attn", "expert"), None),
        P(("attn", "expert"), None),
        P(("attn", "expert"), None),
        P(),
        P(),
        P("expert", None, "attn"),
        P("expert", None, "attn"),
        P("expert", "attn", None),
    )
    out_specs = P(("attn", "expert"), None)
    return jax.shard_map(
        on_device, mesh=mesh, in_specs=in_specs, out_specs=out_specs, check_vma=False
    )
```

time: 227 us -> 99.6 us (0.44)
  waiting for transfers between devices: 99.1 us -> 0 us
  blocking collectives: 82 us -> 0 us
  Pallas kernels: 0 us -> 77.3 us
  matrix products: 24.4 us -> 0 us
  between operations: 14.4 us -> 1.27 us
  local copies, waits for them, and re-layouts: 2.97 us -> 15.2 us
    reduce_scatter x2 -> x0, waiting for transfers between devices: 98.4 us -> none  [the longest x1 64.1 us: on_device(): share = lax.psum_scatter(share, 'attn', scatter_dimension=0, tiled=True)]
    all_gather x2 -> x0, blocking collectives: 82 us -> none  [the longest x1 44.1 us: on_device(): all_ids = lax.all_gather(expert_ids, both, axis=0, tiled=True)]
    pallas_call x0 -> x1, Pallas kernels: none -> 77.3 us  [fused(): pl.pallas_call(kernel, out_shape=jax.ShapeDtypeStruct((rows, width), bf16...]
    dot_general x2 -> x0, matrix products: 24.4 us -> none  [the longest x1 16.3 us: on_device(): jnp.dot(hidden, down_weight[0], preferred_element_type=jnp.float32)]
    unnamed x1 -> x3, local copies, waits for them, and re-layouts: 2.56 us -> 14.6 us
  transfers between devices with their start and end apart: 3 -> 0, of which waited for: 2 -> 0; matrix products, arithmetic and copies ran while one was open for 2% -> 0% of each run, Pallas kernels for 0% -> 0%
where the time goes in v2:
time: 99.6 us; the launch traced here: 99.1 us
  Pallas kernels  77.3 us (78%)
  local copies, waits for them, and re-layouts  15.2 us (15%)
  other arithmetic  5.27 us (5%)
  between operations  1.27 us (1%)
    pallas_call x1, Pallas kernels, fused(): pl.pallas_call(kernel, out_shape=jax.ShapeDtypeStruct((rows, width), bf16...  77.3 us
    unnamed x3, local copies, waits for them, and re-layouts  14.6 us
    reduce_sum x2, other arithmetic, lookup(): jnp.sum(jnp.where(indices[:, None] == places[None, :], table[None, :], 0)...  3.31 us

profile of v2, /device:TPU:0, one launch (start us, length us, event | category | flops | bytes accessed | tf_op | source)
XLA Modules:
  0.0 99.1 jit_solution(5376547967119327103)
XLA Ops:
  0.0 1.3 %fusion.1 = s32[]{:T(128)} fusion(s32[8]{0:T(128)} %param.12, s32[]{:T(128)S(6)} %axis_index.12), kind=kLoop, calls=%fused_computation.8 | loop fusion | flops 23 | bytes 40 | tf_op jit(solution)/shard_map/reduce_sum | solution.py:26
  1.3 2.0 %fusion.2 = (s32[]{:T(128)}, s32[]{:T(128)}) fusion(s32[8]{0:T(128)} %param.11, s32[]{:T(128)} %fusion.1, s32[]{:T(128)S(6)} %axis_index.12), kind=kLoop, calls=%fused_computation.9 | loop fusion | flops 46 | bytes 48 | tf_op jit(solution)/shard_map/reduce_sum | solution.py:26
  4.6 0.6 broadcast_in_dim.9.bound
  5.2 0.7 convert_bitcast_fusion
  5.8 1.3 %select_maximum_fusion.meta = f32[8,128]{1,0:T(8,128)} fusion(f32[4,32]{1,0:T(4,128)} %bitcast.3, f32[4,32]{1,0:T(4,128)S(1)} %convert_bitcast_fusion), kind=kLoop, calls=%fused_computation | loop fusion | flops 5120 | bytes 5120 | tf_op jit(solution)/shard_map/concatenate | solution.py:409
  7.1 6.5 %copy.9.gate_hbm = bf16[1,2880,720]{2,1,0:T(8,128)(2,1)} copy(bf16[1,2880,720]{1,2,0:T(8,128)(2,1)} %param.13) | data formatting | bytes 8294400 | tf_op args[5]
  13.6 6.5 %copy.10.up_hbm = bf16[1,2880,720]{2,1,0:T(8,128)(2,1)} copy(bf16[1,2880,720]{1,2,0:T(8,128)(2,1)} %param.14) | data formatting | bytes 8294400 | tf_op args[6]
  20.1 77.3 %shard_map.82 = bf16[32,2880]{1,0:T(8,128)(2,1)} custom-call(bf16[32,2880]{1,0:T(8,128)(2,1)} %tokens.1, f32[8,128]{1,0:T(8,128)} %select_maximum_fusion.meta, f32[1,128]{1,0:T(1,128)} %broadcast_in_dim.9.bound, bf16[1,2880,720]{2,1,0:T(8,128)(2,1)} %copy.9.gate_hbm, bf16[1,2880,720]{2,1,0:T(8,128)(2,1)} %copy.10.up_hbm, bf16[1,720,2880]{2,1,0:T(8,128)(2,1)} %down_hbm.1), custom_call_target="tpu_custom_call" | custom-call | tf_op jit(solution)/shard_map/pallas_call | solution.py:344
  97.5 1.6 %copy.12 = bf16[32,2880]{1,0:T(8,128)(2,1)} copy(bf16[32,2880]{1,0:T(8,128)(2,1)} %shard_map.82) | data formatting | bytes 368640

commit v3 on v2

--- a/solution.py
+++ b/solution.py
@@ -1,5 +1,3 @@
-import functools
-
 import jax
 import jax.numpy as jnp
 from jax import lax
@@ -41,13 +39,16 @@
 
 def kernel(
     tokens,
-    meta,
-    bound,
+    ids,
+    probs,
+    shed,
+    partner,
     gate_hbm,
     up_hbm,
     down_hbm,
     out,
     x,
+    meta,
     m,
     wcol,
     part,
@@ -61,6 +62,7 @@
     gate,
     up,
     down,
+    hidden,
     send_sem,
     recv_sem,
     load_sem,
@@ -68,7 +70,8 @@
     planes = x.shape[0]
     rows, width = tokens.shape
     half = rows // 2
-    top = meta.shape[0] // 2
+    top = ids.shape[0]
+    capacity = rows * top * x.shape[2]
     a = lax.axis_index("attn")
     e = lax.axis_index("expert")
     z, c = e // 2, e % 2
@@ -172,18 +175,21 @@
         pltpu.make_async_copy(down_hbm.at[0], down, load_sem.at[2]),
     ]
     own.start()
-    own_meta.start()
+    meta[...] = jnp.full(meta.shape, -1.0, jnp.float32)
+    meta[:top, :rows] = ids[...].astype(jnp.float32)
+    meta[top:, :rows] = probs[...]
     for load in loads:
         load.start()
     pl.semaphore_wait(barrier, len(peers))
 
     for s in range(1, planes):
         start(s, META_Z)
+    own_meta.start()
     own.wait()
-    own_meta.wait()
     start(0, OWN_X, OWN_Y, OWN_C)
     for s in range(1, planes):
         start(s, OUT_Z)
+    own_meta.wait()
 
     def stage_own(s):
         arrived(s, OUT_Z)
@@ -204,6 +210,7 @@
         arrived(s, META_A)
     start(0, META_C)
     stage_own(1)
+    stage_own(2)
     arrived(0, META_C)
 
     def row_weights():
@@ -222,7 +229,8 @@
         earlier = jnp.where(j < i, 1.0, 0.0).astype(jnp.bfloat16)
         ahead = jnp.dot(earlier, mask16, preferred_element_type=jnp.float32)
         rank = inside + jnp.sum(ahead, axis=1, keepdims=True)
-        weight = jnp.where(rank < bound[...], prob, 0.0)
+        bound = capacity + capacity // 8 * (shed[e] - shed[partner[e]])
+        weight = jnp.where(rank < bound.astype(jnp.float32), prob, 0.0)
         i = lax.broadcasted_iota(jnp.int32, (rows, LANES), 0)
         j = lax.broadcasted_iota(jnp.int32, (rows, LANES), 1)
         for aa in range(m.shape[0]):
@@ -235,51 +243,53 @@
     row_weights()
     for load in loads:
         load.wait()
-
-    def compute(s):
+    stage_forward(1)
+
+    count = 2 * x.shape[2] * rows
+    along = (((1,), (1,)), ((), ()))
+
+    def compute_hidden(s):
         p = plane(s)
-        count = 2 * m.shape[0] * rows
         xs = x[p].reshape(count, width)
-        gate_part = jnp.dot(xs, gate[...], preferred_element_type=jnp.float32)
-        up_part = jnp.dot(xs, up[...], preferred_element_type=jnp.float32)
-        hidden = activate(gate_part, up_part, wcol[p].reshape(count, 1))
+        gate_part = lax.dot_general(xs, gate[...], along, preferred_element_type=jnp.float32)
+        up_part = lax.dot_general(xs, up[...], along, preferred_element_type=jnp.float32)
+        hidden[...] = activate(gate_part, up_part, wcol[p].reshape(count, 1))
+
+    def compute_share(s):
         step = 8 * LANES
         for first in range(0, width, step):
             cols = slice(first, min(first + step, width))
-            share = jnp.dot(hidden, down[:, cols], preferred_element_type=jnp.float32)
+            share = jnp.dot(hidden[...], down[:, cols], preferred_element_type=jnp.float32)
             part[s, :, :, :, cols] = share.astype(jnp.bfloat16).reshape(
-                2, m.shape[0], rows, cols.stop - cols.start
+                2, x.shape[2], rows, cols.stop - cols.start
             )
+
+    def order(t):
+        return (t + 1) % planes
 
     def body(t, carry):
         @pl.when(t < planes)
         def _():
-            arrived(t, FWD_Y, FWD_X)
-            start(t, PASS_D)
-            arrived(t, OWN_C, PASS_X, PASS_Y, PASS_D)
+            s = order(t)
+            arrived(s, FWD_Y, FWD_X)
+            start(s, PASS_D)
+            arrived(s, OWN_C, PASS_X, PASS_Y, PASS_D)
+
+        @pl.when(t + 3 < planes)
+        def _():
+            stage_own(t + 3)
+
+        @pl.when(t < planes)
+        def _():
+            compute_hidden(order(t))
 
         @pl.when(t + 2 < planes)
         def _():
-            stage_own(t + 2)
-
-        @pl.when(t < planes)
-        def _():
-            compute(t)
-            start(t, SUM_C)
-
-        @pl.when(t + 1 < planes)
-        def _():
-            stage_forward(t + 1)
-
-        @pl.when(t < planes)
-        def _():
-            arrived(t, SUM_C)
-            total[t] = (widen(part.at[t, c]) + widen(core_in.at[t])).astype(jnp.bfloat16)
-            start(t, HALF_X, HALF_Y)
+            stage_forward(t + 2)
 
         @pl.when(jnp.logical_and(t >= 1, t < planes + 1))
         def _():
-            s = t - 1
+            s = order(t - 1)
             arrived(s, HALF_X, HALF_Y)
             low = widen(total.at[s, yn, lo]) + widen(half_in.at[s, 0])
             total[s, yn, lo] = low.astype(jnp.bfloat16)
@@ -288,9 +298,18 @@
             total[s, xn, hi] = high.astype(jnp.bfloat16)
             start(s, FULL_X)
 
+        @pl.when(t < planes)
+        def _():
+            s = order(t)
+            compute_share(s)
+            start(s, SUM_C)
+            arrived(s, SUM_C)
+            total[s] = (widen(part.at[s, c]) + widen(core_in.at[s])).astype(jnp.bfloat16)
+            start(s, HALF_X, HALF_Y)
+
         @pl.when(t >= 2)
         def _():
-            s = t - 2
+            s = order(t - 2)
             arrived(s, FULL_X, FULL_Y)
             value = widen(total.at[s, a]) + widen(full_in.at[s, 0]) + widen(full_in.at[s, 1])
 
@@ -335,20 +354,24 @@
     return weights + planes * group_count * block * (2 + 2 + 1 + 1 + 2) + 12 * 2**20
 
 
-def fused(tokens, meta, bound, gate_weight, up_weight, down_weight, group_count, planes):
+def fused(tokens, ids, probs, shed, partner, gate_weight, up_weight, down_weight, group_count, planes):
     rows, width = tokens.shape
-    hidden = gate_weight.shape[2]
+    hidden = gate_weight.shape[1]
+    count = 2 * group_count * rows
+    table = (2 * ids.shape[0], LANES)
     bf16, f32 = jnp.bfloat16, jnp.float32
     vmem = pl.BlockSpec(memory_space=pltpu.VMEM)
+    smem = pl.BlockSpec(memory_space=pltpu.SMEM)
     hbm = pl.BlockSpec(memory_space=pl.ANY)
     return pl.pallas_call(
         kernel,
         out_shape=jax.ShapeDtypeStruct((rows, width), bf16),
-        in_specs=[vmem, vmem, vmem, hbm, hbm, hbm],
+        in_specs=[vmem, vmem, vmem, smem, smem, hbm, hbm, hbm],
         out_specs=vmem,
         scratch_shapes=[
             pltpu.VMEM((planes, 2, group_count, rows, width), bf16),
-            pltpu.VMEM((group_count, planes, 2) + meta.shape, f32),
+            pltpu.VMEM(table, f32),
+            pltpu.VMEM((group_count, planes, 2) + table, f32),
             pltpu.VMEM((planes, 2, group_count, rows, 1), f32),
             pltpu.VMEM((planes, 2, group_count, rows, width), bf16),
             pltpu.VMEM((planes, group_count, rows, width), bf16),
@@ -358,9 +381,10 @@
             pltpu.VMEM((planes, rows, width), bf16),
             pltpu.VMEM((planes, rows, width), bf16),
             pltpu.VMEM((rows, width), f32),
-            pltpu.VMEM((width, hidden), bf16),
-            pltpu.VMEM((width, hidden), bf16),
             pltpu.VMEM((hidden, width), bf16),
+            pltpu.VMEM((hidden, width), bf16),
+            pltpu.VMEM((hidden, width), bf16),
+            pltpu.VMEM((count, hidden), bf16),
             pltpu.SemaphoreType.DMA((KINDS, planes)),
             pltpu.SemaphoreType.DMA((KINDS, planes)),
             pltpu.SemaphoreType.DMA((5,)),
@@ -368,7 +392,7 @@
         compiler_params=pltpu.CompilerParams(
             collective_id=0, has_side_effects=True, vmem_limit_bytes=VMEM_BYTES
         ),
-    )(tokens, meta, bound, gate_weight, up_weight, down_weight)
+    )(tokens, ids, probs, shed, partner, gate_weight, up_weight, down_weight)
 
 
 def gathered(tokens, expert_ids, gate_probs, bound, gate_weight, up_weight, down_weight):
@@ -396,20 +420,23 @@
     group_count, expert_count = lax.axis_size("attn"), lax.axis_size("expert")
     top_count = expert_ids.shape[1]
     planes = expert_count // 2
-    bound = served_rows(shed_blocks, partner, rows * top_count * group_count)
     fits = fused_bytes(group_count, planes, rows, width, gate_weight.shape[2]) <= VMEM_BYTES
     if group_count != 4 or planes != 4 or rows % 32 or rows > LANES or not fits:
+        bound = served_rows(shed_blocks, partner, rows * top_count * group_count)
         return gathered(
             tokens, expert_ids, gate_probs, bound, gate_weight, up_weight, down_weight
         )
-    ids = jnp.pad(
-        expert_ids.T.astype(jnp.float32), ((0, 0), (0, LANES - rows)), constant_values=-1.0
-    )
-    probs = jnp.pad(gate_probs.T, ((0, 0), (0, LANES - rows)))
-    meta = jnp.concatenate([ids, probs], axis=0)
-    bound = jnp.broadcast_to(bound.astype(jnp.float32)[:, None], (1, LANES))
     return fused(
-        tokens, meta, bound, gate_weight, up_weight, down_weight, group_count, planes
+        tokens,
+        expert_ids.T,
+        gate_probs.T,
+        shed_blocks,
+        partner,
+        jnp.swapaxes(gate_weight, 1, 2),
+        jnp.swapaxes(up_weight, 1, 2),
+        down_weight,
+        group_count,
+        planes,
     )
 
 

time: 99.6 us -> 77.9 us (0.78)
  the two profiles are of different devices: /device:TPU:0 before, /device:TPU:9 now
where the time goes in v3:
time: 77.9 us; the launch traced here: 77.8 us
  Pallas kernels  76.1 us (98%)
  local copies, waits for them, and re-layouts  1.61 us (2%)
    pallas_call x1, Pallas kernels, fused(): pl.pallas_call(kernel, out_shape=jax.ShapeDtypeStruct((rows, width), bf16...  76.1 us
    unnamed x1, local copies, waits for them, and re-layouts  1.61 us

profile of v3, /device:TPU:9, one launch (start us, length us, event | category | flops | bytes accessed | tf_op | source)
XLA Modules:
  0.0 77.8 jit_solution(13792382818791526783)
XLA Ops:
  0.0 76.1 %shard_map.82 = bf16[32,2880]{1,0:T(8,128)(2,1)} custom-call(bf16[32,2880]{1,0:T(8,128)(2,1)} %tokens.1, s32[4,32]{1,0:T(4,128)} %bitcast.6, f32[4,32]{1,0:T(4,128)} %bitcast.7, s32[8]{0:T(128)} %shed.1, s32[8]{0:T(128)} %partner.1, bf16[1,720,2880]{2,1,0:T(8,128)(2,1)} %bitcast.4, bf16[1,720,2880]{2,1,0:T(8,128)(2,1)} %bitcast.5, bf16[1,720,2880]{2,1,0:T(8,128)(2,1)} %down_hbm.1), custom_call_target="tpu_custom_call" | custom-call | tf_op jit(solution)/shard_map/pallas_call | solution.py:366
  76.1 1.6 %copy.10 = bf16[32,2880]{1,0:T(8,128)(2,1)} copy(bf16[32,2880]{1,0:T(8,128)(2,1)} %shard_map.82) | data formatting | bytes 368640
